TPU v7x, 32 devices: a whole 2x2x4 slice. The times are simulated.
32 devices in a mesh: clip: 2 (over y), outer: 4 (over z), inner: 2 (over x), head: 2 (over core).
Axes of the slice: x: 2, y: 2, z: 4, core: 2. Of those that a mesh axis runs over, the one named last changes fastest.
Arguments:
- tokens: bfloat16 [2, 4096, 3072], P('clip', ('outer', 'inner', 'head')), parts along dimension 0, may hold values from -6 to 6
- shift_mod: float32 [2, 3072], P('clip'), parts along dimension 0, may hold values from -3 to 3
- scale_mod: float32 [2, 3072], P('clip'), parts along dimension 0, may hold values from -1.5 to 1.5
- gate_mod: float32 [2, 3072], P('clip'), parts along dimension 0, may hold values from 0.5 to 2
- query_weight: bfloat16 [3072, 3072], P('outer', ('inner', 'head')), may hold values from -0.109375 to 0.109375
- key_weight: bfloat16 [3072, 3072], P('outer', ('inner', 'head')), may hold values from -0.109375 to 0.109375
- value_weight: bfloat16 [3072, 3072], P('outer', ('inner', 'head')), may hold values from -0.109375 to 0.109375
- out_weight: bfloat16 [3072, 3072], P(('inner', 'head'), 'outer'), may hold values from -0.109375 to 0.109375
- query_gain: float32 [128], replicated, may hold values from 1 to 18, as said below
- key_gain: float32 [128], replicated, may hold values from 1 to 18, as said below
Outputs:
- attended: bfloat16 [2, 4096, 3072], P('clip', ('outer', 'inner', 'head')), parts along dimension 0
There are 2 independent parts, one for each index of `clip`. A program takes and returns all parts, laid end to end along the dimension named above; an argument that names none is the same for every part. Nothing has to cross between parts.
Inputs may be any that keep to these rules, and one draw needn't show every extreme that they name: `query_gain`: 128 positive scales. `key_gain`: 128 positive scales.
All inputs are finite; a program needn't handle non-finite values.
Results may differ from a plain program's by a relative error of at most 0.015.
The roundings to bfloat16 on the way count: a program that leaves them out, or rounds other values in their place, can miss the bound.
Values may be sent and summed in bfloat16 or wider, within the bound.
A program may use at most 192 MiB of HBM per device.

v0:
```python
import functools
import math

import jax
import jax.numpy as jnp
from jax import lax
from jax.experimental import pallas as pl
from jax.experimental.pallas import tpu as pltpu
from jax.sharding import PartitionSpec as P

EPSILON = 1e-06


def modulate(tokens, shift_mod, scale_mod):
    values = tokens.astype(jnp.float32)
    center = jnp.mean(values, axis=-1, keepdims=True)
    spread = jnp.mean(jnp.square(values - center), axis=-1, keepdims=True)
    normed = (values - center) / jnp.sqrt(spread + EPSILON)
    return (normed * (1.0 + scale_mod[:, None, :]) + shift_mod[:, None, :]).astype(jnp.bfloat16)


def head_norm(projected, gain_vec, head_dim):
    shaped = projected.reshape(projected.shape[:-1] + (projected.shape[-1] // head_dim, head_dim))
    mean_square = jnp.mean(jnp.square(shaped), axis=-1, keepdims=True)
    return (shaped / jnp.sqrt(mean_square + EPSILON) * gain_vec).astype(jnp.bfloat16)


def per_device(
    tokens,
    shift_mod,
    scale_mod,
    gate_mod,
    query_weight,
    key_weight,
    value_weight,
    out_weight,
    query_gain,
    key_gain,
):
    head_dim = query_gain.shape[0]
    modulated = modulate(tokens, shift_mod, scale_mod)
    gathered = lax.all_gather(modulated, ("inner", "head"), axis=1, tiled=True)
    clip_count, row_count, model_width = gathered.shape
    flattened = gathered.reshape(clip_count * row_count, model_width)
    local_cols = query_weight.shape[1]
    head_count = local_cols // head_dim
    full_query, full_key, full_value = (
        lax.all_gather(query_weight, "outer", axis=0, tiled=True),
        lax.all_gather(key_weight, "outer", axis=0, tiled=True),
        lax.all_gather(value_weight, "outer", axis=0, tiled=True),
    )
    query_proj = jnp.dot(flattened, full_query, preferred_element_type=jnp.float32)
    key_proj = jnp.dot(flattened, full_key, preferred_element_type=jnp.float32)
    value_proj = jnp.dot(flattened, full_value, preferred_element_type=jnp.float32)
    query_heads = head_norm(
        query_proj.reshape(clip_count, row_count, local_cols), query_gain, head_dim
    )
    key_send = head_norm(key_proj.reshape(clip_count, row_count, local_cols), key_gain, head_dim)
    key_send = key_send.reshape(clip_count, row_count, local_cols)
    value_send = value_proj.astype(jnp.bfloat16).reshape(clip_count, row_count, local_cols)
    root_size = math.sqrt(head_dim)
    full_out = lax.all_gather(out_weight, "outer", axis=1, tiled=True)
    running_max = jnp.full((clip_count, head_count, row_count), -1e30, jnp.float32)
    key_piece = lax.all_gather(key_send, "outer", axis=1, tiled=True)
    value_piece = lax.all_gather(value_send, "outer", axis=1, tiled=True)
    key_count = key_piece.shape[1]
    key_piece = key_piece.reshape(clip_count, key_count, head_count, head_dim)
    value_piece = value_piece.reshape(clip_count, key_count, head_count, head_dim)
    scores = (
        jnp.einsum("cqhd,ckhd->chqk", query_heads, key_piece, preferred_element_type=jnp.float32)
        / root_size
    )
    new_max = jnp.maximum(running_max, jnp.max(scores, axis=-1))
    weights = jnp.exp(scores - new_max[..., None])
    new_sum = jnp.sum(weights, axis=-1)
    new_acc = jnp.einsum(
        "chqk,ckhd->chqd",
        weights.astype(jnp.bfloat16),
        value_piece,
        preferred_element_type=jnp.float32,
    )
    head_out = new_acc / new_sum[..., None]
    mixed = (
        jnp.transpose(head_out, (0, 2, 1, 3))
        .reshape(clip_count * row_count, local_cols)
        .astype(jnp.bfloat16)
    )
    partial_value = jnp.dot(mixed, full_out, preferred_element_type=jnp.float32).reshape(
        clip_count, row_count, -1
    )
    summed = lax.psum_scatter(
        partial_value.astype(jnp.bfloat16), ("inner", "head"), scatter_dimension=1, tiled=True
    ).astype(jnp.float32)
    return (summed * gate_mod[:, None, :]).astype(jnp.bfloat16)


def sublayer(
    nz,
    head_dim,
    tokens,
    shift_mod,
    scale_mod,
    gate_mod,
    query_gain,
    key_gain,
    query_weight,
    key_weight,
    value_weight,
    out_weight,
    out,
    weights,
    gathered,
    queries,
    kv,
    out_full,
    mixed,
    staged,
    w_send,
    w_recv,
    wx_send,
    wx_recv,
    wy_send,
    wy_recv,
    t_own,
    t_fwd,
    t_recv,
    s_send,
    s_recv,
    kv_send,
    kv_recv,
    m_send,
    m_recv,
    p_local,
    p_send,
    p_recv,
    o_own,
    o_fwd,
    o_recv,
    oy_send,
    oy_recv,
    ox_send,
    ox_recv,
    od_send,
    od_recv,
    os_send,
    os_recv,
):
    y, z = lax.axis_index("clip"), lax.axis_index("outer")
    x, h = lax.axis_index("inner"), lax.axis_index("head")
    rows, width = tokens.shape
    depth = query_weight.shape[0]
    half = depth // 2
    cols = queries.shape[0] * head_dim
    heads = queries.shape[0]
    per_core = nz // 2
    group, block_cols = out_weight.shape
    group_half = group // 2
    high = z // (nz // 2)
    inner, outer = z + 1 - 2 * high, z - 1 + 2 * high
    middle = jnp.logical_and(z > 0, z < nz - 1)
    end = jnp.logical_not(middle)
    primary = h == x
    other = jnp.logical_not(primary)

    sibling, across_y, across_x = {"head": 1 - h}, {"clip": 1 - y}, {"inner": 1 - x}
    sends = []

    def block(t):
        first, odd = 1 - t // 2, t % 2
        return (
            first * (1 - odd) * z
            + first * odd * (1 - z + 4 * high)
            + (1 - first) * ((1 - high) * t + high * (3 - t))
        )

    def when(cond, run):
        if cond is None:
            run()
        else:
            pl.when(cond)(run)

    def send(src, dst, send_sem, recv_sem, device, cond=None):
        def make():
            return pltpu.make_async_remote_copy(
                src_ref=src(),
                dst_ref=dst(),
                send_sem=send_sem,
                recv_sem=recv_sem,
                device_id=device,
                device_id_type=pl.DeviceIdType.MESH,
            )

        when(cond, lambda: make().start())
        return make

    def post(ref, index, send_sem, recv_sem, device, cond=None, source=None):
        dst = lambda: ref.at[index()]
        src = dst if source is None else source
        made = send(src, dst, send_sem, recv_sem, device, cond)
        sends.append((cond, made))

    def arrive(view, sem):
        pltpu.make_async_copy(view, view, sem).wait()

    barrier = pltpu.get_barrier_semaphore()

    def greet(device):
        pl.semaphore_signal(
            barrier, inc=1, device_id=device, device_id_type=pl.DeviceIdType.MESH
        )

    for zs in range(nz):
        for hs in range(2):
            away = jnp.logical_or(z != zs, h != hs)
            pl.when(away)(lambda zs=zs, hs=hs: greet({"outer": zs, "head": hs}))
    greet(across_y)
    greet(across_x)
    pl.semaphore_wait(barrier, 2 * nz + 1)

    for k in range(per_core):
        target = h * per_core + k
        local = jnp.logical_and(target == z, primary)
        remote = jnp.logical_not(local)
        for m, weight in enumerate((query_weight, key_weight, value_weight)):
            src = weight.at[pl.ds(y * half, half), pl.ds(k * cols, cols)]
            index = (pl.ds(z * depth + y * half, half), pl.ds(m * cols, cols))
            pl.when(local)(
                lambda src=src, index=index, m=m: pltpu.make_async_copy(
                    src, weights.at[index], w_recv.at[z, m]
                ).start()
            )
            post(
                weights,
                lambda index=index: index,
                w_send.at[k, m],
                w_recv.at[z, m],
                {"outer": target, "head": x},
                remote,
                lambda src=src: src,
            )

    own_out = pltpu.make_async_copy(
        out_weight, out_full.at[z, pl.ds((2 * x + h) * group, group)], p_local
    )
    own_out.start()

    slab = 32 if rows % 32 == 0 else 16

    @pl.loop(0, rows // slab)
    def _(r):
        values = tokens[pl.ds(r * slab, slab), :].astype(jnp.float32)
        center = jnp.mean(values, axis=-1, keepdims=True)
        moved = values - center
        spread = jnp.mean(moved * moved, axis=-1, keepdims=True)
        normed = moved * (1.0 / jnp.sqrt(spread + EPSILON))
        changed = normed * (1.0 + scale_mod[...]) + shift_mod[...]
        gathered[z, pl.ds(h * rows + r * slab, slab), :] = changed.astype(jnp.bfloat16)

    def shard(b):
        return lambda: (b, pl.ds(h * rows, rows))

    def sibling_shard(b):
        return gathered.at[b, pl.ds((1 - h) * rows, rows)]

    def near(b):
        return lambda: (pl.ds(b * depth + y * half, half), slice(None))

    def far(b):
        return weights.at[pl.ds(b * depth + (1 - y) * half, half), :]

    b = [block(t) for t in range(nz)]
    post(gathered, shard(z), t_own.at[0], t_recv.at[z], {"outer": inner})
    post(gathered, shard(z), t_own.at[1], t_recv.at[z], {"outer": outer}, middle)
    post(gathered, shard(z), s_send.at[z], s_recv.at[z], sibling)

    def part(bt, gx, gy):
        start = (2 * gx + h) * group + gy * group_half
        return lambda: (bt, pl.ds(start, group_half))

    def out_source():
        return out_weight.at[pl.ds(y * group_half, group_half), :]

    post(
        out_full, part(z, x, y), o_own.at[0], o_recv.at[z], {"outer": inner}, end, out_source
    )

    def pass_on(bt):
        post(weights, near(bt), wy_send.at[bt], wy_recv.at[bt], across_y)

    for bt in b:
        def take(bt=bt):
            for m in range(3):
                index = (pl.ds(bt * depth + y * half, half), pl.ds(m * cols, cols))
                arrive(weights.at[index], w_recv.at[bt, m])

        pl.when(primary)(take)
        post(weights, near(bt), wx_send.at[bt], wx_recv.at[bt], across_x, primary)
        pl.when(other)(lambda bt=bt: arrive(weights.at[near(bt)()], wx_recv.at[bt]))
        pass_on(bt)

    own_index = lambda: (z, pl.ds((2 * x + h) * group, group))
    post(out_full, own_index, p_send.at[0], p_recv.at[0], across_x, None, lambda: out_weight)
    post(out_full, own_index, p_send.at[1], p_recv.at[1], sibling, None, lambda: out_weight)

    def take_tokens(t, cond=None):
        bt = b[t]
        moves = middle if cond is None else jnp.logical_and(middle, cond)
        when(cond, lambda: arrive(gathered.at[shard(bt)()], t_recv.at[bt]))
        target = inner if t == 1 else outer

        def go():
            send(
                lambda: gathered.at[shard(bt)()],
                lambda: gathered.at[shard(bt)()],
                t_fwd.at[t],
                t_recv.at[bt],
                {"outer": target},
            )

        def side():
            send(
                lambda: gathered.at[shard(bt)()],
                lambda: gathered.at[shard(bt)()],
                s_send.at[bt],
                s_recv.at[bt],
                sibling,
            )

        pl.when(moves)(go)
        when(cond, side)

    take_tokens(1)
    post(
        out_full, part(z, x, y), o_own.at[0], o_recv.at[z], {"outer": inner}, middle, out_source
    )
    take_tokens(2, middle)
    for bt in b:
        arrive(far(bt), wy_recv.at[bt])

    def normed_head(projected, gain):
        square = jnp.mean(projected * projected, axis=-1, keepdims=True)
        return (projected * (1.0 / jnp.sqrt(square + EPSILON)) * gain).astype(jnp.bfloat16)

    def project(bt):
        @pl.loop(0, 2)
        def _(r):
            here = pl.ds(pl.multiple_of(r * rows, rows), rows)
            piece = gathered[bt, here, :]
            both = jnp.dot(
                piece, weights[:, : 2 * cols], preferred_element_type=jnp.float32
            )
            for i in range(heads):
                lo = i * head_dim
                queries[i, bt, here, :] = normed_head(
                    both[:, lo : lo + head_dim], query_gain[...]
                )
                kv[0, i, x * nz + bt, here, :] = normed_head(
                    both[:, cols + lo : cols + lo + head_dim], key_gain[...]
                )
            value = jnp.dot(
                piece, weights[:, 2 * cols :], preferred_element_type=jnp.float32
            ).astype(jnp.bfloat16)
            for i in range(heads):
                lo = i * head_dim
                kv[1, i, x * nz + bt, here, :] = value[:, lo : lo + head_dim]

        post(
            kv,
            lambda: (slice(None), slice(None), x * nz + bt),
            kv_send.at[bt],
            kv_recv.at[bt],
            across_x,
        )

    def out_near(t, cond=None):
        bt = b[t]

        def run():
            mine = part(bt, x, y)
            arrive(out_full.at[mine()], o_recv.at[bt])
            target = inner if t == 1 else outer
            view = lambda: out_full.at[mine()]
            pl.when(middle)(
                lambda: send(view, view, o_fwd.at[t], o_recv.at[bt], {"outer": target}) and None
            )
            send(view, view, oy_send.at[t], oy_recv.at[t], across_y)
            send(view, view, ox_send.at[t], ox_recv.at[t], across_x)
            send(view, view, os_send.at[t, 0], os_recv.at[t, 0], sibling)

        when(cond, run)

    def out_second(t):
        bt = b[t]
        side, over = part(bt, x, 1 - y), part(bt, 1 - x, y)
        side_view, over_view = lambda: out_full.at[side()], lambda: out_full.at[over()]
        arrive(side_view(), oy_recv.at[t])
        if t == 1:
            send(side_view, side_view, od_send.at[t], od_recv.at[t], across_x)
        send(side_view, side_view, os_send.at[t, 1], os_recv.at[t, 1], sibling)
        arrive(over_view(), ox_recv.at[t])
        if t > 1:
            send(over_view, over_view, od_send.at[t], od_recv.at[t], across_y)
        send(over_view, over_view, os_send.at[t, 2], os_recv.at[t, 2], sibling)

    def out_third(t):
        last = part(b[t], 1 - x, 1 - y)
        view = lambda: out_full.at[last()]
        arrive(view(), od_recv.at[t])
        send(view, view, os_send.at[t, 3], os_recv.at[t, 3], sibling)

    arrive(sibling_shard(b[0]), s_recv.at[b[0]])
    project(b[0])
    arrive(sibling_shard(b[1]), s_recv.at[b[1]])
    project(b[1])
    take_tokens(2, end)
    arrive(sibling_shard(b[2]), s_recv.at[b[2]])
    project(b[2])
    take_tokens(3)
    post(
        out_full, part(z, x, y), o_own.at[1], o_recv.at[z], {"outer": outer}, middle, out_source
    )
    out_near(1, middle)
    cross = lambda: (z, pl.ds((2 * (1 - x) + h) * group, group))
    arrive(out_full.at[cross()], p_recv.at[0])
    post(out_full, cross, p_send.at[2], p_recv.at[2], sibling)
    arrive(sibling_shard(b[3]), s_recv.at[b[3]])
    project(b[3])
    for bt in b:
        arrive(kv.at[:, :, (1 - x) * nz + bt], kv_recv.at[bt])

    factor = math.log2(math.e) / math.sqrt(head_dim)
    key_blocks, key_rows = kv.shape[2], kv.shape[3]
    span = 2 if key_blocks % 2 == 0 else 1

    def attend_rows(query, i):
        total = None
        for c in range(0, key_blocks, span):
            keys = kv[0, i, c : c + span].reshape(span * key_rows, head_dim)
            values = kv[1, i, c : c + span].reshape(span * key_rows, head_dim)
            scores = lax.dot_general(
                query, keys, (((1,), (1,)), ((), ())), preferred_element_type=jnp.float32
            )
            peak = jnp.max(scores, axis=-1, keepdims=True)
            if c:
                peak = jnp.maximum(top, peak)
            probs = jnp.exp2((scores - peak) * factor)
            fresh = jnp.sum(probs, axis=-1, keepdims=True)
            gained = jnp.dot(
                probs.astype(jnp.bfloat16), values, preferred_element_type=jnp.float32
            )
            if c:
                shrink = jnp.exp2((top - peak) * factor)
                total, result = total * shrink + fresh, result * shrink + gained
            else:
                total, result = fresh, gained
            top = peak
        return (result / total).astype(jnp.bfloat16)

    def place():
        return (slice(None), pl.ds((h * nz + z) * cols, cols))

    duties = {
        1: lambda: (out_near(1, end), out_near(2, middle)),
        3: lambda: (out_near(2, end), out_near(3, middle), out_second(1)),
        5: lambda: (out_near(3, end), out_second(2), out_third(1)),
        7: lambda: (out_second(3), out_third(2)),
    }

    @pl.loop(0, 2 * nz)
    def _(j):
        for at, duty in duties.items():
            pl.when(j == at)(lambda duty=duty: duty() and None)
        bt = block(nz - 1 - j // 2)
        core = (j % 2) * h + (1 - j % 2) * (1 - h)

        @pl.loop(0, heads)
        def _(i):
            query = queries[i, bt, pl.ds(core * rows, rows), :]
            staged[bt, core, :, pl.ds(pl.multiple_of(i * head_dim, head_dim), head_dim)] = (
                attend_rows(query, i)
            )

        self_place = jnp.logical_and(bt == z, core == h)

        def keep():
            mixed[place()] = staged[bt, core]

        pl.when(self_place)(keep)

        def give():
            send(
                lambda: staged.at[bt, core],
                lambda: mixed.at[place()],
                m_send.at[bt, core],
                m_recv.at[h * nz + z],
                {"outer": bt, "head": core},
            )

        pl.when(jnp.logical_not(self_place))(give)

    out_third(3)
    for zs in range(nz):
        for hs in range(2):
            k = hs * nz + zs
            pl.when(jnp.logical_or(z != zs, h != hs))(
                lambda k=k: arrive(mixed.at[:, k * cols : (k + 1) * cols], m_recv.at[k])
            )

    def sibling_part(bt, gx, gy):
        start = (2 * gx + 1 - h) * group + gy * group_half
        return out_full.at[bt, pl.ds(start, group_half)]

    own_out.wait()
    for gx, n in ((x, 1), (1 - x, 2)):
        arrive(out_full.at[z, pl.ds((2 * gx + 1 - h) * group, group)], p_recv.at[n])

    for t in range(nz):
        bt = b[t]
        if t:
            for n, (gx, gy) in enumerate(((x, y), (x, 1 - y), (1 - x, y), (1 - x, 1 - y))):
                arrive(sibling_part(bt, gx, gy), os_recv.at[t, n])
        summed = jnp.zeros((rows, block_cols), jnp.float32)
        for g in range(4):
            term = jnp.dot(
                mixed[:, g * group : (g + 1) * group],
                out_full[bt, g * group : (g + 1) * group, :],
                preferred_element_type=jnp.float32,
            )
            summed = summed + term.astype(jnp.bfloat16).astype(jnp.float32)
        here = pl.ds(pl.multiple_of(bt * block_cols, block_cols), block_cols)
        out[:, here] = (summed * gate_mod[:, here]).astype(jnp.bfloat16)

    for cond, made in sends:
        when(cond, lambda made=made: made().wait_send())

    def sent(view, sem):
        pltpu.make_async_copy(view, view, sem).wait()

    for t in range(1, nz):
        bt = b[t]
        tok = gathered.at[shard(bt)()]
        pl.when(middle)(lambda tok=tok, t=t: sent(tok, t_fwd.at[t]))
        sent(tok, s_send.at[bt])
        piece = out_full.at[part(bt, x, y)()]
        pl.when(middle)(lambda piece=piece, t=t: sent(piece, o_fwd.at[t]))
        sent(piece, oy_send.at[t])
        sent(piece, ox_send.at[t])
        sent(piece, od_send.at[t])
        for n in range(4):
            sent(piece, os_send.at[t, n])
    for zs in range(nz):
        for hs in range(2):
            pl.when(jnp.logical_or(z != zs, h != hs))(
                lambda zs=zs, hs=hs: sent(staged.at[zs, hs], m_send.at[zs, hs])
            )


def fused(nz, tokens, shift_mod, scale_mod, gate_mod, *rest):
    wq, wk, wv, wo, query_gain, key_gain = rest
    _, rows, width = tokens.shape
    head_dim = query_gain.shape[0]
    depth, group_cols = wq.shape
    heads = 4 * group_cols // head_dim // (2 * nz)
    cols = heads * head_dim
    dma = lambda *shape: pltpu.SemaphoreType.DMA(shape)
    vmem = pl.BlockSpec(memory_space=pltpu.VMEM)
    anywhere = pl.BlockSpec(memory_space=pl.ANY)
    result = pl.pallas_call(
        functools.partial(sublayer, nz, head_dim),
        out_shape=jax.ShapeDtypeStruct((rows, width), jnp.bfloat16),
        in_specs=[vmem] * 6 + [anywhere] * 4,
        out_specs=vmem,
        scratch_shapes=[
            pltpu.VMEM((width, 3 * cols), jnp.bfloat16),
            pltpu.VMEM((nz, 2 * rows, width), jnp.bfloat16),
            pltpu.VMEM((heads, nz, 2 * rows, head_dim), jnp.bfloat16),
            pltpu.VMEM((2, heads, 2 * nz, 2 * rows, head_dim), jnp.bfloat16),
            pltpu.VMEM((nz, 4 * wo.shape[0], wo.shape[1]), jnp.bfloat16),
            pltpu.VMEM((rows, width), jnp.bfloat16),
            pltpu.VMEM((nz, 2, rows, cols), jnp.bfloat16),
            dma(nz // 2, 3),
            dma(nz, 3),
            dma(nz),
            dma(nz),
            dma(nz),
            dma(nz),
            dma(2),
            dma(nz),
            dma(nz),
            dma(nz),
            dma(nz),
            dma(nz),
            dma(nz),
            dma(nz, 2),
            dma(2 * nz),
            pltpu.SemaphoreType.DMA,
            dma(3),
            dma(3),
            dma(2),
            dma(nz),
            dma(nz),
            dma(nz),
            dma(nz),
            dma(nz),
            dma(nz),
            dma(nz),
            dma(nz),
            dma(nz, 4),
            dma(nz, 4),
        ],
        compiler_params=pltpu.CompilerParams(
            collective_id=0, has_side_effects=True, vmem_limit_bytes=67043328
        ),
        name="sublayer",
    )(
        tokens[0],
        shift_mod,
        scale_mod,
        gate_mod,
        query_gain[None],
        key_gain[None],
        wq,
        wk,
        wv,
        wo,
    )
    return result[None]


def fits(mesh, args):
    sizes = mesh.shape
    head_dim, (depth, group_cols) = args[8].shape[0], args[4].shape
    nz = sizes["outer"]
    return (
        sizes["inner"] == 2
        and sizes["head"] == 2
        and sizes["clip"] == 2
        and nz == 4
        and args[0].shape[0] == 1
        and args[0].shape[1] % 16 == 0
        and head_dim % 128 == 0
        and (4 * group_cols) % (2 * nz * head_dim) == 0
        and depth % 32 == 0
    )


def solution(mesh):
    in_specs = (
        P("clip", ("outer", "inner", "head"), None),
        P("clip", None),
        P("clip", None),
        P("clip", None),
        P("outer", ("inner", "head")),
        P("outer", ("inner", "head")),
        P("outer", ("inner", "head")),
        P(("inner", "head"), "outer"),
        P(),
        P(),
    )
    out_specs = P("clip", ("outer", "inner", "head"), None)

    def body(*args):
        if fits(mesh, args):
            return fused(mesh.shape["outer"], *args)
        return per_device(*args)

    return jax.shard_map(
        body, mesh=mesh, in_specs=in_specs, out_specs=out_specs, check_vma=False
    )
```

profile of v0, /device:TPU:1, one launch (start us, length us, event | category | flops | bytes accessed | tf_op | source)
XLA Modules:
  0.0 271.4 jit_solution(2526961374560570798)
XLA Ops:
  0.0 268.7 %sublayer.1 = bf16[256,3072]{1,0:T(8,128)(2,1)} custom-call(bf16[256,3072]{1,0:T(8,128)(2,1)} %bitcast.5, f32[1,3072]{1,0:T(1,128)} %shift_mod.1, f32[1,3072]{1,0:T(1,128)} %scale_mod.1, f32[1,3072]{1,0:T(1,128)} %gate_mod.1, f32[1,128]{1,0:T(1,128)} %bitcast.6, f32[1,128]{1,0:T(1,128)} %bitcast.7, bf16[768,768]{1,0:T(8,128)(2,1)} %query_weight.1, ...), custom_call_target="tpu_custom_call" | custom-call | tf_op jit(solution)/shard_map/sublayer/pallas_call | solution.py:568
  268.7 2.7 copy.12
where the time goes:
time: 272 us; the launch traced here: 271 us
  Pallas kernels  269 us (99%)
    pallas_call x1, Pallas kernels, fused(): pl.pallas_call(functools.partial(sublayer, nz, head_dim), out_shape=jax.S...  269 us

commit v1 on v0

--- a/solution.py
+++ b/solution.py
@@ -215,36 +215,15 @@
             pl.when(away)(lambda zs=zs, hs=hs: greet({"outer": zs, "head": hs}))
     greet(across_y)
     greet(across_x)
-    pl.semaphore_wait(barrier, 2 * nz + 1)
-
-    for k in range(per_core):
-        target = h * per_core + k
-        local = jnp.logical_and(target == z, primary)
-        remote = jnp.logical_not(local)
-        for m, weight in enumerate((query_weight, key_weight, value_weight)):
-            src = weight.at[pl.ds(y * half, half), pl.ds(k * cols, cols)]
-            index = (pl.ds(z * depth + y * half, half), pl.ds(m * cols, cols))
-            pl.when(local)(
-                lambda src=src, index=index, m=m: pltpu.make_async_copy(
-                    src, weights.at[index], w_recv.at[z, m]
-                ).start()
-            )
-            post(
-                weights,
-                lambda index=index: index,
-                w_send.at[k, m],
-                w_recv.at[z, m],
-                {"outer": target, "head": x},
-                remote,
-                lambda src=src: src,
-            )
-
     own_out = pltpu.make_async_copy(
         out_weight, out_full.at[z, pl.ds((2 * x + h) * group, group)], p_local
     )
     own_out.start()
 
-    slab = 32 if rows % 32 == 0 else 16
+    chunks = gathered.shape[1]
+    piece_rows = rows // chunks
+    slab = 32 if piece_rows % 32 == 0 else 16 if piece_rows % 16 == 0 else 8
+    per_chunk = piece_rows // slab
 
     @pl.loop(0, rows // slab)
     def _(r):
@@ -254,25 +233,51 @@
         spread = jnp.mean(moved * moved, axis=-1, keepdims=True)
         normed = moved * (1.0 / jnp.sqrt(spread + EPSILON))
         changed = normed * (1.0 + scale_mod[...]) + shift_mod[...]
-        gathered[z, pl.ds(h * rows + r * slab, slab), :] = changed.astype(jnp.bfloat16)
-
-    def shard(b):
-        return lambda: (b, pl.ds(h * rows, rows))
-
-    def sibling_shard(b):
-        return gathered.at[b, pl.ds((1 - h) * rows, rows)]
-
-    def near(b):
-        return lambda: (pl.ds(b * depth + y * half, half), slice(None))
-
-    def far(b):
-        return weights.at[pl.ds(b * depth + (1 - y) * half, half), :]
+        gathered[z, r // per_chunk, h, pl.ds((r % per_chunk) * slab, slab), :] = (
+            changed.astype(jnp.bfloat16)
+        )
+
+    pl.semaphore_wait(barrier, 2 * nz + 1)
+
+    for n in range(per_core):
+        k = n + h * (per_core - 1 - 2 * n)
+        target = h * per_core + k
+        here, away = target == z, target != z
+        local = jnp.logical_and(here, primary)
+        beside = jnp.logical_and(here, other)
+        for m, weight in enumerate((query_weight, key_weight, value_weight)):
+            taken = pl.ds(pl.multiple_of(k * cols, cols), cols)
+            whole = (pl.ds(z * depth, depth), pl.ds(m * cols, cols))
+            piece = (pl.ds(z * depth + y * half, half), pl.ds(m * cols, cols))
+            full_src = weight.at[:, taken]
+            half_src = weight.at[pl.ds(y * half, half), taken]
+            pl.when(local)(
+                lambda src=full_src, index=whole, m=m: pltpu.make_async_copy(
+                    src, weights.at[index], w_recv.at[z, m]
+                ).start()
+            )
+            for cond, src, index in ((beside, full_src, whole), (away, half_src, piece)):
+                post(
+                    weights,
+                    lambda index=index: index,
+                    w_send.at[n, m],
+                    w_recv.at[z, m],
+                    {"outer": target, "head": x},
+                    cond,
+                    lambda src=src: src,
+                )
+
+    def shard(bt, c):
+        return lambda: (bt, c, h)
+
+    def near(t):
+        start = b[t] * depth + (y * half if t else 0)
+        return lambda: (pl.ds(start, half if t else depth), slice(None))
+
+    def far(bt, m):
+        return weights.at[pl.ds(bt * depth + (1 - y) * half, half), pl.ds(m * cols, cols)]
 
     b = [block(t) for t in range(nz)]
-    post(gathered, shard(z), t_own.at[0], t_recv.at[z], {"outer": inner})
-    post(gathered, shard(z), t_own.at[1], t_recv.at[z], {"outer": outer}, middle)
-    post(gathered, shard(z), s_send.at[z], s_recv.at[z], sibling)
-
     def part(bt, gx, gy):
         start = (2 * gx + h) * group + gy * group_half
         return lambda: (bt, pl.ds(start, group_half))
@@ -280,81 +285,89 @@
     def out_source():
         return out_weight.at[pl.ds(y * group_half, group_half), :]
 
-    post(
-        out_full, part(z, x, y), o_own.at[0], o_recv.at[z], {"outer": inner}, end, out_source
-    )
-
-    def pass_on(bt):
-        post(weights, near(bt), wy_send.at[bt], wy_recv.at[bt], across_y)
-
-    for bt in b:
-        def take(bt=bt):
-            for m in range(3):
-                index = (pl.ds(bt * depth + y * half, half), pl.ds(m * cols, cols))
-                arrive(weights.at[index], w_recv.at[bt, m])
-
-        pl.when(primary)(take)
-        post(weights, near(bt), wx_send.at[bt], wx_recv.at[bt], across_x, primary)
-        pl.when(other)(lambda bt=bt: arrive(weights.at[near(bt)()], wx_recv.at[bt]))
-        pass_on(bt)
-
+    def own_out_to(n, target, cond):
+        post(
+            out_full, part(z, x, y), o_own.at[n], o_recv.at[z], {"outer": target}, cond, out_source
+        )
+
+    def give_tokens():
+        for c in range(chunks):
+            post(gathered, shard(z, c), t_own.at[0, c], t_recv.at[z, c], {"outer": inner})
+            post(gathered, shard(z, c), t_own.at[1, c], t_recv.at[z, c], {"outer": outer}, middle)
+        own_out_to(0, inner, end)
+        own_out_to(1, outer, middle)
+        for c in range(chunks):
+            post(gathered, shard(z, c), s_send.at[z, c], s_recv.at[z, c], sibling)
+
+    for t in range(nz):
+        for m in range(3):
+            index = lambda t=t, m=m: (near(t)()[0], pl.ds(m * cols, cols))
+            view = weights.at[index()]
+            pl.when(primary)(lambda: arrive(view, w_recv.at[b[t], m]))
+            post(weights, index, wx_send.at[t, m], wx_recv.at[t, m], across_x, primary)
+            pl.when(other)(lambda: arrive(view, wx_recv.at[t, m]))
+            if t:
+                post(weights, index, wy_send.at[t, m], wy_recv.at[t, m], across_y)
+        if t == 1:
+            give_tokens()
+
+    post(out_full, part(z, x, y), p_send.at[0], p_recv.at[0], across_x, None, out_source)
     own_index = lambda: (z, pl.ds((2 * x + h) * group, group))
-    post(out_full, own_index, p_send.at[0], p_recv.at[0], across_x, None, lambda: out_weight)
     post(out_full, own_index, p_send.at[1], p_recv.at[1], sibling, None, lambda: out_weight)
 
     def take_tokens(t, cond=None):
         bt = b[t]
         moves = middle if cond is None else jnp.logical_and(middle, cond)
-        when(cond, lambda: arrive(gathered.at[shard(bt)()], t_recv.at[bt]))
         target = inner if t == 1 else outer
-
-        def go():
-            send(
-                lambda: gathered.at[shard(bt)()],
-                lambda: gathered.at[shard(bt)()],
-                t_fwd.at[t],
-                t_recv.at[bt],
-                {"outer": target},
-            )
-
-        def side():
-            send(
-                lambda: gathered.at[shard(bt)()],
-                lambda: gathered.at[shard(bt)()],
-                s_send.at[bt],
-                s_recv.at[bt],
-                sibling,
-            )
-
-        pl.when(moves)(go)
-        when(cond, side)
-
-    take_tokens(1)
-    post(
-        out_full, part(z, x, y), o_own.at[0], o_recv.at[z], {"outer": inner}, middle, out_source
-    )
-    take_tokens(2, middle)
-    for bt in b:
-        arrive(far(bt), wy_recv.at[bt])
+        return [take_chunk(t, c, bt, cond, moves, target) for c in range(chunks)]
+
+    def take_chunk(t, c, bt, cond, moves, target):
+        view = lambda: gathered.at[shard(bt, c)()]
+
+        def run():
+            when(cond, lambda: arrive(view(), t_recv.at[bt, c]))
+            pl.when(moves)(
+                lambda: send(view, view, t_fwd.at[t, c], t_recv.at[bt, c], {"outer": target})
+                and None
+            )
+            when(
+                cond,
+                lambda: send(view, view, s_send.at[bt, c], s_recv.at[bt, c], sibling) and None,
+            )
+
+        return run
+
+    for one, two in zip(take_tokens(1), take_tokens(2, middle)):
+        one()
+        two()
+    own_out_to(0, inner, middle)
+    for t in range(1, nz):
+        for m in range(3):
+            arrive(far(b[t], m), wy_recv.at[t, m])
+
+    def beside(bt, c):
+        arrive(gathered.at[bt, c, 1 - h], s_recv.at[bt, c])
 
     def normed_head(projected, gain):
         square = jnp.mean(projected * projected, axis=-1, keepdims=True)
         return (projected * (1.0 / jnp.sqrt(square + EPSILON)) * gain).astype(jnp.bfloat16)
 
-    def project(bt):
-        @pl.loop(0, 2)
-        def _(r):
-            here = pl.ds(pl.multiple_of(r * rows, rows), rows)
-            piece = gathered[bt, here, :]
+    def project(bt, before=()):
+        def piece_of(c):
+            piece = gathered[bt, c].reshape(2 * piece_rows, width)
+            spot = pl.ds(pl.multiple_of(c * 2 * piece_rows, 2 * piece_rows), 2 * piece_rows)
+            mine = pl.ds(pl.multiple_of(c * piece_rows, piece_rows), piece_rows)
             both = jnp.dot(
                 piece, weights[:, : 2 * cols], preferred_element_type=jnp.float32
             )
             for i in range(heads):
                 lo = i * head_dim
-                queries[i, bt, here, :] = normed_head(
-                    both[:, lo : lo + head_dim], query_gain[...]
-                )
-                kv[0, i, x * nz + bt, here, :] = normed_head(
+                query = normed_head(both[:, lo : lo + head_dim], query_gain[...])
+                for core in range(2):
+                    queries[i, bt, core, mine, :] = query[
+                        core * piece_rows : (core + 1) * piece_rows
+                    ]
+                kv[0, i, x * nz + bt, spot, :] = normed_head(
                     both[:, cols + lo : cols + lo + head_dim], key_gain[...]
                 )
             value = jnp.dot(
@@ -362,15 +375,16 @@
             ).astype(jnp.bfloat16)
             for i in range(heads):
                 lo = i * head_dim
-                kv[1, i, x * nz + bt, here, :] = value[:, lo : lo + head_dim]
-
-        post(
-            kv,
-            lambda: (slice(None), slice(None), x * nz + bt),
-            kv_send.at[bt],
-            kv_recv.at[bt],
-            across_x,
-        )
+                kv[1, i, x * nz + bt, spot, :] = value[:, lo : lo + head_dim]
+            view = lambda: kv.at[:, :, x * nz + bt, spot]
+            send(view, view, kv_send.at[bt, c], kv_recv.at[bt, c], across_x)
+
+        @pl.loop(0, chunks)
+        def _(c):
+            for n, step in enumerate(before):
+                pl.when(c == n)(step)
+            beside(bt, c)
+            piece_of(c)
 
     def out_near(t, cond=None):
         bt = b[t]
@@ -394,11 +408,11 @@
         side, over = part(bt, x, 1 - y), part(bt, 1 - x, y)
         side_view, over_view = lambda: out_full.at[side()], lambda: out_full.at[over()]
         arrive(side_view(), oy_recv.at[t])
-        if t == 1:
+        if t == nz - 1:
             send(side_view, side_view, od_send.at[t], od_recv.at[t], across_x)
         send(side_view, side_view, os_send.at[t, 1], os_recv.at[t, 1], sibling)
         arrive(over_view(), ox_recv.at[t])
-        if t > 1:
+        if t < nz - 1:
             send(over_view, over_view, od_send.at[t], od_recv.at[t], across_y)
         send(over_view, over_view, os_send.at[t, 2], os_recv.at[t, 2], sibling)
 
@@ -408,38 +422,40 @@
         arrive(view(), od_recv.at[t])
         send(view, view, os_send.at[t, 3], os_recv.at[t, 3], sibling)
 
-    arrive(sibling_shard(b[0]), s_recv.at[b[0]])
     project(b[0])
-    arrive(sibling_shard(b[1]), s_recv.at[b[1]])
     project(b[1])
-    take_tokens(2, end)
-    arrive(sibling_shard(b[2]), s_recv.at[b[2]])
-    project(b[2])
-    take_tokens(3)
-    post(
-        out_full, part(z, x, y), o_own.at[1], o_recv.at[z], {"outer": outer}, middle, out_source
-    )
-    out_near(1, middle)
-    cross = lambda: (z, pl.ds((2 * (1 - x) + h) * group, group))
-    arrive(out_full.at[cross()], p_recv.at[0])
-    post(out_full, cross, p_send.at[2], p_recv.at[2], sibling)
-    arrive(sibling_shard(b[3]), s_recv.at[b[3]])
-    project(b[3])
-    for bt in b:
-        arrive(kv.at[:, :, (1 - x) * nz + bt], kv_recv.at[bt])
+    out_near(1)
+    crossed = part(z, 1 - x, y)
+    arrive(out_full.at[crossed()], p_recv.at[0])
+    post(out_full, crossed, od_send.at[0], od_recv.at[0], across_y)
+    post(out_full, crossed, os_send.at[0, 2], os_recv.at[0, 2], sibling)
+    project(b[2], take_tokens(2, end))
+    project(b[3], take_tokens(3))
+    out_near(2, middle)
+    out_near(3, middle)
+    out_second(1)
+    out_third(0)
+    for t in range(nz):
+        for c in range(chunks):
+            spot = pl.ds(c * 2 * piece_rows, 2 * piece_rows)
+            arrive(kv.at[:, :, (1 - x) * nz + b[t], spot], kv_recv.at[b[t], c])
 
     factor = math.log2(math.e) / math.sqrt(head_dim)
     key_blocks, key_rows = kv.shape[2], kv.shape[3]
     span = 2 if key_blocks % 2 == 0 else 1
 
     def attend_rows(query, i):
-        total = None
+        def score(c):
+            keys = kv[0, i, c : c + span].reshape(span * key_rows, head_dim)
+            return lax.dot_general(
+                query, keys, (((1,), (1,)), ((), ())), preferred_element_type=jnp.float32
+            )
+
+        total = result = top = None
+        scores = score(0)
         for c in range(0, key_blocks, span):
-            keys = kv[0, i, c : c + span].reshape(span * key_rows, head_dim)
+            after = score(c + span) if c + span < key_blocks else None
             values = kv[1, i, c : c + span].reshape(span * key_rows, head_dim)
-            scores = lax.dot_general(
-                query, keys, (((1,), (1,)), ((), ())), preferred_element_type=jnp.float32
-            )
             peak = jnp.max(scores, axis=-1, keepdims=True)
             if c:
                 peak = jnp.maximum(top, peak)
@@ -453,51 +469,50 @@
                 total, result = total * shrink + fresh, result * shrink + gained
             else:
                 total, result = fresh, gained
-            top = peak
+            top, scores = peak, after
         return (result / total).astype(jnp.bfloat16)
 
     def place():
         return (slice(None), pl.ds((h * nz + z) * cols, cols))
 
     duties = {
-        1: lambda: (out_near(1, end), out_near(2, middle)),
-        3: lambda: (out_near(2, end), out_near(3, middle), out_second(1)),
-        5: lambda: (out_near(3, end), out_second(2), out_third(1)),
-        7: lambda: (out_second(3), out_third(2)),
+        0: lambda: (out_near(2, end), out_third(1)),
+        1: lambda: out_near(3, end),
+        2: lambda: out_second(2),
+        3: lambda: out_second(3),
     }
 
-    @pl.loop(0, 2 * nz)
+    @pl.loop(0, nz)
     def _(j):
         for at, duty in duties.items():
             pl.when(j == at)(lambda duty=duty: duty() and None)
-        bt = block(nz - 1 - j // 2)
-        core = (j % 2) * h + (1 - j % 2) * (1 - h)
+        bt = block(nz - 1 - j)
 
         @pl.loop(0, heads)
         def _(i):
-            query = queries[i, bt, pl.ds(core * rows, rows), :]
-            staged[bt, core, :, pl.ds(pl.multiple_of(i * head_dim, head_dim), head_dim)] = (
-                attend_rows(query, i)
-            )
-
-        self_place = jnp.logical_and(bt == z, core == h)
-
-        def keep():
-            mixed[place()] = staged[bt, core]
-
-        pl.when(self_place)(keep)
-
-        def give():
-            send(
-                lambda: staged.at[bt, core],
-                lambda: mixed.at[place()],
-                m_send.at[bt, core],
-                m_recv.at[h * nz + z],
-                {"outer": bt, "head": core},
-            )
-
-        pl.when(jnp.logical_not(self_place))(give)
-
+            query = queries[i, bt].reshape(2 * rows, head_dim)
+            spot = pl.ds(pl.multiple_of(i * head_dim, head_dim), head_dim)
+            staged[bt, :, :, spot] = attend_rows(query, i).reshape(2, rows, head_dim)
+
+        for core in range(2):
+            self_place = jnp.logical_and(bt == z, h == core)
+
+            def keep():
+                mixed[place()] = staged[bt, core]
+
+            def give():
+                send(
+                    lambda: staged.at[bt, core],
+                    lambda: mixed.at[place()],
+                    m_send.at[bt, core],
+                    m_recv.at[h * nz + z],
+                    {"outer": bt, "head": core},
+                )
+
+            pl.when(self_place)(keep)
+            pl.when(jnp.logical_not(self_place))(give)
+
+    out_third(2)
     out_third(3)
     for zs in range(nz):
         for hs in range(2):
@@ -511,13 +526,12 @@
         return out_full.at[bt, pl.ds(start, group_half)]
 
     own_out.wait()
-    for gx, n in ((x, 1), (1 - x, 2)):
-        arrive(out_full.at[z, pl.ds((2 * gx + 1 - h) * group, group)], p_recv.at[n])
+    arrive(out_full.at[z, pl.ds((2 * x + 1 - h) * group, group)], p_recv.at[1])
 
     for t in range(nz):
         bt = b[t]
-        if t:
-            for n, (gx, gy) in enumerate(((x, y), (x, 1 - y), (1 - x, y), (1 - x, 1 - y))):
+        for n, (gx, gy) in enumerate(((x, y), (x, 1 - y), (1 - x, y), (1 - x, 1 - y))):
+            if t or n > 1:
                 arrive(sibling_part(bt, gx, gy), os_recv.at[t, n])
         summed = jnp.zeros((rows, block_cols), jnp.float32)
         for g in range(4):
@@ -536,18 +550,24 @@
     def sent(view, sem):
         pltpu.make_async_copy(view, view, sem).wait()
 
-    for t in range(1, nz):
+    for t in range(nz):
         bt = b[t]
-        tok = gathered.at[shard(bt)()]
-        pl.when(middle)(lambda tok=tok, t=t: sent(tok, t_fwd.at[t]))
-        sent(tok, s_send.at[bt])
         piece = out_full.at[part(bt, x, y)()]
-        pl.when(middle)(lambda piece=piece, t=t: sent(piece, o_fwd.at[t]))
-        sent(piece, oy_send.at[t])
-        sent(piece, ox_send.at[t])
-        sent(piece, od_send.at[t])
+        for c in range(chunks):
+            tok = gathered.at[shard(bt, c)()]
+            spot = pl.ds(c * 2 * piece_rows, 2 * piece_rows)
+            sent(kv.at[:, :, x * nz + bt, spot], kv_send.at[bt, c])
+            if t:
+                pl.when(middle)(lambda tok=tok, t=t, c=c: sent(tok, t_fwd.at[t, c]))
+                sent(tok, s_send.at[bt, c])
+        if t:
+            pl.when(middle)(lambda piece=piece, t=t: sent(piece, o_fwd.at[t]))
+            sent(piece, oy_send.at[t])
+            sent(piece, ox_send.at[t])
+            sent(piece, od_send.at[t])
         for n in range(4):
-            sent(piece, os_send.at[t, n])
+            if t or n > 2:
+                sent(piece, os_send.at[t, n])
     for zs in range(nz):
         for hs in range(2):
             pl.when(jnp.logical_or(z != zs, h != hs))(
@@ -562,6 +582,7 @@
     depth, group_cols = wq.shape
     heads = 4 * group_cols // head_dim // (2 * nz)
     cols = heads * head_dim
+    chunks = 2
     dma = lambda *shape: pltpu.SemaphoreType.DMA(shape)
     vmem = pl.BlockSpec(memory_space=pltpu.VMEM)
     anywhere = pl.BlockSpec(memory_space=pl.ANY)
@@ -572,30 +593,30 @@
         out_specs=vmem,
         scratch_shapes=[
             pltpu.VMEM((width, 3 * cols), jnp.bfloat16),
-            pltpu.VMEM((nz, 2 * rows, width), jnp.bfloat16),
-            pltpu.VMEM((heads, nz, 2 * rows, head_dim), jnp.bfloat16),
+            pltpu.VMEM((nz, chunks, 2, rows // chunks, width), jnp.bfloat16),
+            pltpu.VMEM((heads, nz, 2, rows, head_dim), jnp.bfloat16),
             pltpu.VMEM((2, heads, 2 * nz, 2 * rows, head_dim), jnp.bfloat16),
             pltpu.VMEM((nz, 4 * wo.shape[0], wo.shape[1]), jnp.bfloat16),
             pltpu.VMEM((rows, width), jnp.bfloat16),
             pltpu.VMEM((nz, 2, rows, cols), jnp.bfloat16),
             dma(nz // 2, 3),
             dma(nz, 3),
-            dma(nz),
-            dma(nz),
-            dma(nz),
-            dma(nz),
-            dma(2),
-            dma(nz),
-            dma(nz),
-            dma(nz),
-            dma(nz),
-            dma(nz),
-            dma(nz),
+            dma(nz, 3),
+            dma(nz, 3),
+            dma(nz, 3),
+            dma(nz, 3),
+            dma(2, chunks),
+            dma(nz, chunks),
+            dma(nz, chunks),
+            dma(nz, chunks),
+            dma(nz, chunks),
+            dma(nz, chunks),
+            dma(nz, chunks),
             dma(nz, 2),
             dma(2 * nz),
             pltpu.SemaphoreType.DMA,
-            dma(3),
-            dma(3),
+            dma(2),
+            dma(2),
             dma(2),
             dma(nz),
             dma(nz),
@@ -637,7 +658,7 @@
         and sizes["clip"] == 2
         and nz == 4
         and args[0].shape[0] == 1
-        and args[0].shape[1] % 16 == 0
+        and args[0].shape[1] % 32 == 0
         and head_dim % 128 == 0
         and (4 * group_cols) % (2 * nz * head_dim) == 0
         and depth % 32 == 0

time: 272 us -> 228 us (0.84)
  Pallas kernels: 269 us -> 225 us
    pallas_call x1, Pallas kernels: 269 us -> 225 us  [fused(): pl.pallas_call(functools.partial(sublayer, nz, head_dim), out_shape=jax.S...]
where the time goes in v1:
time: 228 us; the launch traced here: 227 us
  Pallas kernels  225 us (99%)
  local copies, waits for them, and re-layouts  2.65 us (1%)
    pallas_call x1, Pallas kernels, fused(): pl.pallas_call(functools.partial(sublayer, nz, head_dim), out_shape=jax.S...  225 us

profile of v1, /device:TPU:1, one launch (start us, length us, event | category | flops | bytes accessed | tf_op | source)
XLA Modules:
  0.0 227.4 jit_solution(5467836315152053421)
XLA Ops:
  0.0 224.8 %sublayer.1 = bf16[256,3072]{1,0:T(8,128)(2,1)} custom-call(bf16[256,3072]{1,0:T(8,128)(2,1)} %bitcast.5, f32[1,3072]{1,0:T(1,128)} %shift_mod.1, f32[1,3072]{1,0:T(1,128)} %scale_mod.1, f32[1,3072]{1,0:T(1,128)} %gate_mod.1, f32[1,128]{1,0:T(1,128)} %bitcast.6, f32[1,128]{1,0:T(1,128)} %bitcast.7, bf16[768,768]{1,0:T(8,128)(2,1)} %query_weight.1, ...), custom_call_target="tpu_custom_call" | custom-call | tf_op jit(solution)/shard_map/sublayer/pallas_call | solution.py:589
  224.8 2.7 %copy.12 = bf16[1,256,3072]{2,1,0:T(8,128)(2,1)} copy(bf16[1,256,3072]{2,1,0:T(8,128)(2,1)} %bitcast.4) | data formatting | bytes 3145728

commit v2 on v1

--- a/solution.py
+++ b/solution.py
@@ -114,7 +114,7 @@
     kv,
     out_full,
     mixed,
-    staged,
+    state,
     w_send,
     w_recv,
     wx_send,
@@ -144,6 +144,7 @@
     od_recv,
     os_send,
     os_recv,
+    fetched,
 ):
     y, z = lax.axis_index("clip"), lax.axis_index("outer")
     x, h = lax.axis_index("inner"), lax.axis_index("head")
@@ -202,6 +203,9 @@
     def arrive(view, sem):
         pltpu.make_async_copy(view, view, sem).wait()
 
+    fetch = pltpu.make_async_copy(tokens, out, fetched)
+    fetch.start()
+
     barrier = pltpu.get_barrier_semaphore()
 
     def greet(device):
@@ -215,28 +219,6 @@
             pl.when(away)(lambda zs=zs, hs=hs: greet({"outer": zs, "head": hs}))
     greet(across_y)
     greet(across_x)
-    own_out = pltpu.make_async_copy(
-        out_weight, out_full.at[z, pl.ds((2 * x + h) * group, group)], p_local
-    )
-    own_out.start()
-
-    chunks = gathered.shape[1]
-    piece_rows = rows // chunks
-    slab = 32 if piece_rows % 32 == 0 else 16 if piece_rows % 16 == 0 else 8
-    per_chunk = piece_rows // slab
-
-    @pl.loop(0, rows // slab)
-    def _(r):
-        values = tokens[pl.ds(r * slab, slab), :].astype(jnp.float32)
-        center = jnp.mean(values, axis=-1, keepdims=True)
-        moved = values - center
-        spread = jnp.mean(moved * moved, axis=-1, keepdims=True)
-        normed = moved * (1.0 / jnp.sqrt(spread + EPSILON))
-        changed = normed * (1.0 + scale_mod[...]) + shift_mod[...]
-        gathered[z, r // per_chunk, h, pl.ds((r % per_chunk) * slab, slab), :] = (
-            changed.astype(jnp.bfloat16)
-        )
-
     pl.semaphore_wait(barrier, 2 * nz + 1)
 
     for n in range(per_core):
@@ -267,6 +249,29 @@
                     lambda src=src: src,
                 )
 
+    own_out = pltpu.make_async_copy(
+        out_weight, out_full.at[z, pl.ds((2 * x + h) * group, group)], p_local
+    )
+    own_out.start()
+
+    fetch.wait()
+    chunks = gathered.shape[1]
+    piece_rows = rows // chunks
+    slab = 32 if piece_rows % 32 == 0 else 16 if piece_rows % 16 == 0 else 8
+    per_chunk = piece_rows // slab
+
+    @pl.loop(0, rows // slab)
+    def _(r):
+        values = out[pl.ds(r * slab, slab), :].astype(jnp.float32)
+        center = jnp.mean(values, axis=-1, keepdims=True)
+        moved = values - center
+        spread = jnp.mean(moved * moved, axis=-1, keepdims=True)
+        normed = moved * (1.0 / jnp.sqrt(spread + EPSILON))
+        changed = normed * (1.0 + scale_mod[...]) + shift_mod[...]
+        gathered[z, r // per_chunk, h, pl.ds((r % per_chunk) * slab, slab), :] = (
+            changed.astype(jnp.bfloat16)
+        )
+
     def shard(bt, c):
         return lambda: (bt, c, h)
 
@@ -282,13 +287,27 @@
         start = (2 * gx + h) * group + gy * group_half
         return lambda: (bt, pl.ds(start, group_half))
 
+    def quarter(bt, gx, gy, c):
+        size = group_half // 2
+        start = (2 * gx + h) * group + gy * group_half + c * size
+        return lambda: (bt, pl.ds(start, size))
+
     def out_source():
         return out_weight.at[pl.ds(y * group_half, group_half), :]
 
     def own_out_to(n, target, cond):
-        post(
-            out_full, part(z, x, y), o_own.at[n], o_recv.at[z], {"outer": target}, cond, out_source
-        )
+        for c in range(2):
+            size = group_half // 2
+            source = out_weight.at[pl.ds(y * group_half + c * size, size), :]
+            post(
+                out_full,
+                quarter(z, x, y, c),
+                o_own.at[n, c],
+                o_recv.at[z, c],
+                {"outer": target},
+                cond,
+                lambda source=source: source,
+            )
 
     def give_tokens():
         for c in range(chunks):
@@ -367,7 +386,7 @@
                     queries[i, bt, core, mine, :] = query[
                         core * piece_rows : (core + 1) * piece_rows
                     ]
-                kv[0, i, x * nz + bt, spot, :] = normed_head(
+                kv[0, i, 2 * bt + x, spot, :] = normed_head(
                     both[:, cols + lo : cols + lo + head_dim], key_gain[...]
                 )
             value = jnp.dot(
@@ -375,8 +394,8 @@
             ).astype(jnp.bfloat16)
             for i in range(heads):
                 lo = i * head_dim
-                kv[1, i, x * nz + bt, spot, :] = value[:, lo : lo + head_dim]
-            view = lambda: kv.at[:, :, x * nz + bt, spot]
+                kv[1, i, 2 * bt + x, spot, :] = value[:, lo : lo + head_dim]
+            view = lambda: kv.at[:, :, 2 * bt + x, spot]
             send(view, view, kv_send.at[bt, c], kv_recv.at[bt, c], across_x)
 
         @pl.loop(0, chunks)
@@ -386,134 +405,198 @@
             beside(bt, c)
             piece_of(c)
 
-    def out_near(t, cond=None):
+    def out_near(t, cond=None, pieces=(0, 1)):
         bt = b[t]
 
         def run():
-            mine = part(bt, x, y)
-            arrive(out_full.at[mine()], o_recv.at[bt])
-            target = inner if t == 1 else outer
-            view = lambda: out_full.at[mine()]
-            pl.when(middle)(
-                lambda: send(view, view, o_fwd.at[t], o_recv.at[bt], {"outer": target}) and None
-            )
-            send(view, view, oy_send.at[t], oy_recv.at[t], across_y)
-            send(view, view, ox_send.at[t], ox_recv.at[t], across_x)
-            send(view, view, os_send.at[t, 0], os_recv.at[t, 0], sibling)
+            for c in pieces:
+                mine = quarter(bt, x, y, c)
+                view = lambda: out_full.at[mine()]
+                arrive(view(), o_recv.at[bt, c])
+                target = inner if t == 1 else outer
+                pl.when(middle)(
+                    lambda: send(view, view, o_fwd.at[t, c], o_recv.at[bt, c], {"outer": target})
+                    and None
+                )
+                send(view, view, oy_send.at[t, c], oy_recv.at[t, c], across_y)
+                send(view, view, ox_send.at[t, c], ox_recv.at[t, c], across_x)
+                send(view, view, os_send.at[t, c], os_recv.at[t, c], sibling)
 
         when(cond, run)
 
-    def out_second(t):
+    def out_second(t, pieces=(0, 1)):
         bt = b[t]
-        side, over = part(bt, x, 1 - y), part(bt, 1 - x, y)
-        side_view, over_view = lambda: out_full.at[side()], lambda: out_full.at[over()]
-        arrive(side_view(), oy_recv.at[t])
-        if t == nz - 1:
-            send(side_view, side_view, od_send.at[t], od_recv.at[t], across_x)
-        send(side_view, side_view, os_send.at[t, 1], os_recv.at[t, 1], sibling)
-        arrive(over_view(), ox_recv.at[t])
-        if t < nz - 1:
-            send(over_view, over_view, od_send.at[t], od_recv.at[t], across_y)
-        send(over_view, over_view, os_send.at[t, 2], os_recv.at[t, 2], sibling)
+        for c in pieces:
+            side, over = quarter(bt, x, 1 - y, c), quarter(bt, 1 - x, y, c)
+            side_view, over_view = lambda: out_full.at[side()], lambda: out_full.at[over()]
+            arrive(side_view(), oy_recv.at[t, c])
+            if t > 1 and c:
+                send(side_view, side_view, od_send.at[t, c], od_recv.at[t, c], across_x)
+            send(side_view, side_view, os_send.at[t, 2 + c], os_recv.at[t, 2 + c], sibling)
+            arrive(over_view(), ox_recv.at[t, c])
+            if t == 1 or not c:
+                send(over_view, over_view, od_send.at[t, c], od_recv.at[t, c], across_y)
+            send(over_view, over_view, os_send.at[t, 4 + c], os_recv.at[t, 4 + c], sibling)
 
     def out_third(t):
-        last = part(b[t], 1 - x, 1 - y)
-        view = lambda: out_full.at[last()]
-        arrive(view(), od_recv.at[t])
-        send(view, view, os_send.at[t, 3], os_recv.at[t, 3], sibling)
+        if t == 0:
+            last = part(z, 1 - x, 1 - y)
+            view = lambda: out_full.at[last()]
+            arrive(view(), od_recv.at[0, 0])
+            send(view, view, os_send.at[0, 1], os_recv.at[0, 1], sibling)
+            return
+        for c in range(2):
+            last = quarter(b[t], 1 - x, 1 - y, c)
+            view = lambda: out_full.at[last()]
+            arrive(view(), od_recv.at[t, c])
+            send(view, view, os_send.at[t, 6 + c], os_recv.at[t, 6 + c], sibling)
+
+    factor = math.log2(math.e) / math.sqrt(head_dim)
+    key_rows = kv.shape[3]
+
+    def score(query, i, bt):
+        keys = kv[0, i, pl.ds(2 * bt, 2)].reshape(2 * key_rows, head_dim)
+        return lax.dot_general(
+            query, keys, (((1,), (1,)), ((), ())), preferred_element_type=jnp.float32
+        )
+
+    def wide(column, times):
+        return jnp.concatenate([column] * times, axis=1)
+
+    def fold(carry, scores, i, bt):
+        values = kv[1, i, pl.ds(2 * bt, 2)].reshape(2 * key_rows, head_dim)
+        shape = (scores.shape[0], head_dim)
+        peak = jnp.broadcast_to(jnp.max(scores, axis=-1, keepdims=True), shape)
+        if carry is not None:
+            top, total, result = carry
+            peak = jnp.maximum(top, peak)
+        times = scores.shape[1] // head_dim
+        probs = jnp.exp2((scores - wide(peak, times)) * factor)
+        fresh = jnp.broadcast_to(jnp.sum(probs, axis=-1, keepdims=True), shape)
+        gained = jnp.dot(
+            probs.astype(jnp.bfloat16), values, preferred_element_type=jnp.float32
+        )
+        if carry is None:
+            return peak, fresh, gained
+        shrink = jnp.exp2((top - peak) * factor)
+        return peak, total * shrink + fresh, result * shrink + gained
+
+    def query_of(i, bt):
+        return queries[i, bt].reshape(2 * rows, head_dim)
+
+    def keep_state(u, i, carry):
+        for n, value in enumerate(carry):
+            state[n, u, i] = value
+
+    def load_state(u, i):
+        return [state[n, u, i] for n in range(3)]
+
+    def finish(i, bt, carry):
+        _, total, result = carry
+        queries[i, bt] = (result / total).astype(jnp.bfloat16).reshape(2, rows, head_dim)
+
+    def first_pass(t, bt, done, duty=None):
+        @pl.loop(0, heads)
+        def _(i):
+            if duty is not None:
+                duty(i)
+            query = query_of(i, bt)
+            carry, scores = None, score(query, i, b[0])
+            for n in range(t + 1):
+                after = score(query, i, b[n + 1]) if n < t else None
+                carry = fold(carry, scores, i, b[n])
+                scores = after
+            done(i, carry)
+
+    def later_pass(u, bt, bk):
+        carried = [load_state(u, i) for i in range(heads)]
+        scores = score(query_of(0, bt), 0, bk)
+        ends = []
+        for i in range(heads):
+            after = score(query_of(i + 1, bt), i + 1, bk) if i + 1 < heads else None
+            ends.append(fold(carried[i], scores, i, bk))
+            scores = after
+        for i in range(heads):
+            finish(i, bt, ends[i])
+
+    def keys_arrive(t):
+        for c in range(chunks):
+            spot = pl.ds(c * 2 * piece_rows, 2 * piece_rows)
+            arrive(kv.at[:, :, 2 * b[t] + 1 - x, spot], kv_recv.at[b[t], c])
+
+    def ahead():
+        for t in range(nz - 1):
+            keys_arrive(t)
+
+        @pl.loop(0, 2)
+        def _(u):
+            pl.when(u == 1)(lambda: out_near(2, end, (0,)))
+            first_pass(nz - 2, block(u + 1), lambda i, carry: keep_state(u, i, carry))
+
+    def place(i):
+        start = (h * nz + z) * cols + i * head_dim
+        return (slice(None), pl.ds(pl.multiple_of(start, head_dim), head_dim))
+
+    def hand_over(bt):
+        for core in range(2):
+            self_place = jnp.logical_and(bt == z, h == core)
+
+            def keep():
+                for i in range(heads):
+                    mixed[place(i)] = queries[i, bt, core]
+
+            def give():
+                for i in range(heads):
+                    send(
+                        lambda: queries.at[i, bt, core],
+                        lambda: mixed.at[place(i)],
+                        m_send.at[bt, core],
+                        m_recv.at[h * nz + z],
+                        {"outer": bt, "head": core},
+                    )
+
+            pl.when(self_place)(keep)
+            pl.when(jnp.logical_not(self_place))(give)
 
     project(b[0])
     project(b[1])
     out_near(1)
     crossed = part(z, 1 - x, y)
     arrive(out_full.at[crossed()], p_recv.at[0])
-    post(out_full, crossed, od_send.at[0], od_recv.at[0], across_y)
-    post(out_full, crossed, os_send.at[0, 2], os_recv.at[0, 2], sibling)
+    post(out_full, crossed, od_send.at[0, 0], od_recv.at[0, 0], across_y)
+    post(out_full, crossed, os_send.at[0, 0], os_recv.at[0, 0], sibling)
     project(b[2], take_tokens(2, end))
     project(b[3], take_tokens(3))
     out_near(2, middle)
     out_near(3, middle)
     out_second(1)
     out_third(0)
-    for t in range(nz):
-        for c in range(chunks):
-            spot = pl.ds(c * 2 * piece_rows, 2 * piece_rows)
-            arrive(kv.at[:, :, (1 - x) * nz + b[t], spot], kv_recv.at[b[t], c])
-
-    factor = math.log2(math.e) / math.sqrt(head_dim)
-    key_blocks, key_rows = kv.shape[2], kv.shape[3]
-    span = 2 if key_blocks % 2 == 0 else 1
-
-    def attend_rows(query, i):
-        def score(c):
-            keys = kv[0, i, c : c + span].reshape(span * key_rows, head_dim)
-            return lax.dot_general(
-                query, keys, (((1,), (1,)), ((), ())), preferred_element_type=jnp.float32
-            )
-
-        total = result = top = None
-        scores = score(0)
-        for c in range(0, key_blocks, span):
-            after = score(c + span) if c + span < key_blocks else None
-            values = kv[1, i, c : c + span].reshape(span * key_rows, head_dim)
-            peak = jnp.max(scores, axis=-1, keepdims=True)
-            if c:
-                peak = jnp.maximum(top, peak)
-            probs = jnp.exp2((scores - peak) * factor)
-            fresh = jnp.sum(probs, axis=-1, keepdims=True)
-            gained = jnp.dot(
-                probs.astype(jnp.bfloat16), values, preferred_element_type=jnp.float32
-            )
-            if c:
-                shrink = jnp.exp2((top - peak) * factor)
-                total, result = total * shrink + fresh, result * shrink + gained
-            else:
-                total, result = fresh, gained
-            top, scores = peak, after
-        return (result / total).astype(jnp.bfloat16)
-
-    def place():
-        return (slice(None), pl.ds((h * nz + z) * cols, cols))
-
-    duties = {
-        0: lambda: (out_near(2, end), out_third(1)),
-        1: lambda: out_near(3, end),
-        2: lambda: out_second(2),
-        3: lambda: out_second(3),
-    }
-
-    @pl.loop(0, nz)
-    def _(j):
-        for at, duty in duties.items():
-            pl.when(j == at)(lambda duty=duty: duty() and None)
-        bt = block(nz - 1 - j)
-
-        @pl.loop(0, heads)
-        def _(i):
-            query = queries[i, bt].reshape(2 * rows, head_dim)
-            spot = pl.ds(pl.multiple_of(i * head_dim, head_dim), head_dim)
-            staged[bt, :, :, spot] = attend_rows(query, i).reshape(2, rows, head_dim)
-
-        for core in range(2):
-            self_place = jnp.logical_and(bt == z, h == core)
-
-            def keep():
-                mixed[place()] = staged[bt, core]
-
-            def give():
-                send(
-                    lambda: staged.at[bt, core],
-                    lambda: mixed.at[place()],
-                    m_send.at[bt, core],
-                    m_recv.at[h * nz + z],
-                    {"outer": bt, "head": core},
-                )
-
-            pl.when(self_place)(keep)
-            pl.when(jnp.logical_not(self_place))(give)
-
+    ahead()
+    out_near(2, end, (1,))
+    keys_arrive(3)
+    later_pass(0, b[1], b[3])
+    hand_over(b[1])
+    later_pass(1, b[2], b[3])
+    hand_over(b[2])
+    out_third(1)
+    soon = min(1, heads - 1)
+    first_pass(
+        3,
+        b[3],
+        lambda i, carry: finish(i, b[3], carry),
+        lambda i: pl.when(i == soon)(lambda: out_near(3, end, (0,))),
+    )
+    hand_over(b[3])
+    out_near(3, end, (1,))
+    first_pass(
+        3,
+        b[0],
+        lambda i, carry: finish(i, b[0], carry),
+        lambda i: pl.when(i == soon)(lambda: out_second(2)),
+    )
+    hand_over(b[0])
+    out_second(3)
     out_third(2)
-    out_third(3)
     for zs in range(nz):
         for hs in range(2):
             k = hs * nz + zs
@@ -521,18 +604,25 @@
                 lambda k=k: arrive(mixed.at[:, k * cols : (k + 1) * cols], m_recv.at[k])
             )
 
-    def sibling_part(bt, gx, gy):
-        start = (2 * gx + 1 - h) * group + gy * group_half
-        return out_full.at[bt, pl.ds(start, group_half)]
+    def sibling_part(bt, gx, gy, c):
+        size = group_half if c is None else group_half // 2
+        start = (2 * gx + 1 - h) * group + gy * group_half + (c or 0) * size
+        return out_full.at[bt, pl.ds(start, size)]
 
     own_out.wait()
     arrive(out_full.at[z, pl.ds((2 * x + 1 - h) * group, group)], p_recv.at[1])
 
     for t in range(nz):
         bt = b[t]
-        for n, (gx, gy) in enumerate(((x, y), (x, 1 - y), (1 - x, y), (1 - x, 1 - y))):
-            if t or n > 1:
-                arrive(sibling_part(bt, gx, gy), os_recv.at[t, n])
+        if t == nz - 2:
+            out_third(nz - 1)
+        if t:
+            for n, (gx, gy) in enumerate(((x, y), (x, 1 - y), (1 - x, y), (1 - x, 1 - y))):
+                for c in range(2):
+                    arrive(sibling_part(bt, gx, gy, c), os_recv.at[t, 2 * n + c])
+        else:
+            for n in range(2):
+                arrive(sibling_part(z, 1 - x, y + n - 2 * n * y, None), os_recv.at[0, n])
         summed = jnp.zeros((rows, block_cols), jnp.float32)
         for g in range(4):
             term = jnp.dot(
@@ -552,26 +642,27 @@
 
     for t in range(nz):
         bt = b[t]
-        piece = out_full.at[part(bt, x, y)()]
+        piece = out_full.at[quarter(bt, x, y, 0)()]
         for c in range(chunks):
             tok = gathered.at[shard(bt, c)()]
             spot = pl.ds(c * 2 * piece_rows, 2 * piece_rows)
-            sent(kv.at[:, :, x * nz + bt, spot], kv_send.at[bt, c])
+            sent(kv.at[:, :, 2 * bt + x, spot], kv_send.at[bt, c])
             if t:
                 pl.when(middle)(lambda tok=tok, t=t, c=c: sent(tok, t_fwd.at[t, c]))
                 sent(tok, s_send.at[bt, c])
         if t:
-            pl.when(middle)(lambda piece=piece, t=t: sent(piece, o_fwd.at[t]))
-            sent(piece, oy_send.at[t])
-            sent(piece, ox_send.at[t])
-            sent(piece, od_send.at[t])
-        for n in range(4):
-            if t or n > 2:
+            for c in range(2):
+                pl.when(middle)(lambda piece=piece, t=t, c=c: sent(piece, o_fwd.at[t, c]))
+                sent(piece, oy_send.at[t, c])
+                sent(piece, ox_send.at[t, c])
+                sent(piece, od_send.at[t, c])
+            for n in range(8):
                 sent(piece, os_send.at[t, n])
+    sent(out_full.at[part(z, x, y)()], os_send.at[0, 1])
     for zs in range(nz):
         for hs in range(2):
             pl.when(jnp.logical_or(z != zs, h != hs))(
-                lambda zs=zs, hs=hs: sent(staged.at[zs, hs], m_send.at[zs, hs])
+                lambda zs=zs, hs=hs: sent(queries.at[:, zs, hs], m_send.at[zs, hs])
             )
 
 
@@ -589,7 +680,7 @@
     result = pl.pallas_call(
         functools.partial(sublayer, nz, head_dim),
         out_shape=jax.ShapeDtypeStruct((rows, width), jnp.bfloat16),
-        in_specs=[vmem] * 6 + [anywhere] * 4,
+        in_specs=[anywhere] + [vmem] * 5 + [anywhere] * 4,
         out_specs=vmem,
         scratch_shapes=[
             pltpu.VMEM((width, 3 * cols), jnp.bfloat16),
@@ -598,7 +689,7 @@
             pltpu.VMEM((2, heads, 2 * nz, 2 * rows, head_dim), jnp.bfloat16),
             pltpu.VMEM((nz, 4 * wo.shape[0], wo.shape[1]), jnp.bfloat16),
             pltpu.VMEM((rows, width), jnp.bfloat16),
-            pltpu.VMEM((nz, 2, rows, cols), jnp.bfloat16),
+            pltpu.VMEM((3, 2, heads, 2 * rows, head_dim), jnp.float32),
             dma(nz // 2, 3),
             dma(nz, 3),
             dma(nz, 3),
@@ -617,17 +708,18 @@
             pltpu.SemaphoreType.DMA,
             dma(2),
             dma(2),
-            dma(2),
-            dma(nz),
-            dma(nz),
-            dma(nz),
-            dma(nz),
-            dma(nz),
-            dma(nz),
-            dma(nz),
-            dma(nz),
-            dma(nz, 4),
-            dma(nz, 4),
+            dma(2, 2),
+            dma(nz, 2),
+            dma(nz, 2),
+            dma(nz, 2),
+            dma(nz, 2),
+            dma(nz, 2),
+            dma(nz, 2),
+            dma(nz, 2),
+            dma(nz, 2),
+            dma(nz, 8),
+            dma(nz, 8),
+            pltpu.SemaphoreType.DMA,
         ],
         compiler_params=pltpu.CompilerParams(
             collective_id=0, has_side_effects=True, vmem_limit_bytes=67043328
@@ -659,6 +751,7 @@
         and nz == 4
         and args[0].shape[0] == 1
         and args[0].shape[1] % 32 == 0
+        and args[7].shape[0] % 64 == 0
         and head_dim % 128 == 0
         and (4 * group_cols) % (2 * nz * head_dim) == 0
         and depth % 32 == 0

time: 228 us -> 222 us (0.974)
  Pallas kernels: 225 us -> 219 us
    pallas_call x1, Pallas kernels: 225 us -> 219 us  [fused(): pl.pallas_call(functools.partial(sublayer, nz, head_dim), out_shape=jax.S...]
where the time goes in v2:
time: 222 us; the launch traced here: 221 us
  Pallas kernels  219 us (99%)
  local copies, waits for them, and re-layouts  2.65 us (1%)
    pallas_call x1, Pallas kernels, fused(): pl.pallas_call(functools.partial(sublayer, nz, head_dim), out_shape=jax.S...  219 us

profile of v2, /device:TPU:1, one launch (start us, length us, event | category | flops | bytes accessed | tf_op | source)
XLA Modules:
  0.0 221.2 jit_solution(16027161907257663720)
XLA Ops:
  0.0 218.5 %sublayer.1 = bf16[256,3072]{1,0:T(8,128)(2,1)} custom-call(bf16[256,3072]{1,0:T(8,128)(2,1)} %bitcast.5, f32[1,3072]{1,0:T(1,128)} %shift_mod.1, f32[1,3072]{1,0:T(1,128)} %scale_mod.1, f32[1,3072]{1,0:T(1,128)} %gate_mod.1, f32[1,128]{1,0:T(1,128)} %bitcast.6, f32[1,128]{1,0:T(1,128)} %bitcast.7, bf16[768,768]{1,0:T(8,128)(2,1)} %query_weight.1, ...), custom_call_target="tpu_custom_call" | custom-call | tf_op jit(solution)/shard_map/sublayer/pallas_call | solution.py:680
  218.5 2.7 %copy.12 = bf16[1,256,3072]{2,1,0:T(8,128)(2,1)} copy(bf16[1,256,3072]{2,1,0:T(8,128)(2,1)} %bitcast.4) | data formatting | bytes 3145728
